TPU v7x, 32 devices: a whole 2x2x4 slice. The times are simulated.
32 devices in a mesh: rows: 8 (over z, x), grp: 4 (over y, core).
Axes of the slice: x: 2, y: 2, z: 4, core: 2. Of those that a mesh axis runs over, the one named last changes fastest.
Arguments:
- tiles: bfloat16 [4096, 128, 128], P(('rows', 'grp')), may hold values from -0.3125 to 0.3125
- tile_rows: int32 [4096], P(('rows', 'grp')), may hold values from 0 to 47, as said below
- tile_cols: int32 [4096], P(('rows', 'grp')), may hold values from 0 to 511, as said below
- tile_count: int32 [32], P(('rows', 'grp')), may hold values from 32 to 128, as said below
- block_perm: int32 [512], replicated, may hold values from 0 to 511, as said below
- panel: bfloat16 [512, 128, 256], P(('rows', 'grp')), may hold values from -6 to 6
Outputs:
- sketch: bfloat16 [1536, 128, 256], P(('rows', 'grp'))
- gram: float32 [512, 128, 256], P(('rows', 'grp'))
Inputs may be any that keep to these rules, and one draw needn't show every extreme that they name: `tile_rows`: each device's live tile rows are non-decreasing; slots past the count hold 47. `tile_cols`: among one device's live tiles, those whose block_perm positions lie with one owner (position // 16) name at most 2 distinct column blocks; every device reaches 2 for some owner. `tile_count`: some device has 128 live tiles. `block_perm`: A permutation of the column blocks.
All inputs are finite; a program needn't handle non-finite values.
Results may differ from a plain program's by a relative error of at most 0.0034.
Values may be sent and summed in bfloat16 or wider, within the bound.
A program may use at most 128 MiB of HBM per device.

v0:
```python
import jax
import jax.numpy as jnp
from jax import lax
from jax.sharding import PartitionSpec as P

RB_DEV = 48
PAIR_CAP = 2


def rank_blocks(needed, held_blocks):
    ranking = jnp.cumsum(needed.astype(jnp.int32), axis=-1) - 1
    local_ids = jnp.arange(held_blocks, dtype=jnp.int32)
    listed = [
        jnp.max(jnp.where(needed & (ranking == slot), local_ids, -1), axis=-1)
        for slot in range(PAIR_CAP)
    ]
    return (ranking, jnp.stack(listed, axis=-1))


def per_device(tiles, tile_rows, tile_cols, tile_count, block_perm, panel):
    devices = lax.axis_size(("rows", "grp"))
    tile_slots = tiles.shape[0]
    held_blocks = panel.shape[0]
    slot_ids = jnp.arange(tile_slots, dtype=jnp.int32)
    is_live = slot_ids < tile_count[0]
    stored_at = block_perm[tile_cols]
    owner_of = stored_at // held_blocks
    local_block = stored_at % held_blocks
    positions = jnp.arange(devices * held_blocks, dtype=jnp.int32)
    needed = jnp.any(is_live[:, None] & (stored_at[:, None] == positions[None, :]), axis=0).reshape(
        devices, held_blocks
    )
    ranking, wanted = rank_blocks(needed, held_blocks)
    asked_for = lax.all_to_all(wanted, ("rows", "grp"), split_axis=0, concat_axis=0, tiled=True)
    outgoing = panel[jnp.maximum(asked_for, 0)]
    fetched = lax.all_to_all(outgoing, ("rows", "grp"), split_axis=0, concat_axis=0, tiled=True)
    slot_of = owner_of * PAIR_CAP + ranking[owner_of, local_block]
    slot_of = jnp.where(is_live, slot_of, 0)
    per_tile = fetched.reshape((devices * PAIR_CAP,) + fetched.shape[2:])[slot_of]
    product = jnp.einsum("tij,tjk->tik", tiles, per_tile, preferred_element_type=jnp.float32)
    row_ids = jnp.where(is_live, tile_rows, RB_DEV)
    sketch = jax.ops.segment_sum(product, row_ids, num_segments=RB_DEV).astype(jnp.bfloat16)
    partial_value = jnp.einsum(
        "tij,tik->tjk", tiles, sketch[tile_rows], preferred_element_type=jnp.float32
    )
    slot_rows = jnp.where(is_live, slot_of, devices * PAIR_CAP)
    outbound = jax.ops.segment_sum(
        partial_value, slot_rows, num_segments=devices * PAIR_CAP
    ).astype(jnp.bfloat16)
    outbound = outbound.reshape(outgoing.shape)
    inbound = lax.all_to_all(outbound, ("rows", "grp"), split_axis=0, concat_axis=0, tiled=True)
    flat_in = inbound.reshape((devices * PAIR_CAP,) + inbound.shape[2:])
    block_hot = (
        asked_for.reshape(-1)[None, :] == jnp.arange(held_blocks, dtype=jnp.int32)[:, None]
    ).astype(jnp.bfloat16)
    gram = jnp.einsum("bs,sjk->bjk", block_hot, flat_in, preferred_element_type=jnp.float32)
    return (sketch, gram)


def solution(mesh):
    return jax.shard_map(
        per_device,
        mesh=mesh,
        in_specs=(
            P(("rows", "grp"), None, None),
            P(("rows", "grp")),
            P(("rows", "grp")),
            P(("rows", "grp")),
            P(),
            P(("rows", "grp"), None, None),
        ),
        out_specs=(P(("rows", "grp"), None, None), P(("rows", "grp"), None, None)),
        check_vma=False,
    )
```

profile of v0, /device:TPU:0, one launch (start us, length us, event | category | flops | bytes accessed | tf_op | source)
XLA Modules:
  0.0 416.9 jit_solution(8743284422210854104)
XLA Ops:
  0.6 0.7 compare_select_fusion.4
  2.1 1.6 gather_fusion
  3.7 0.1 fusion.1
  3.9 0.2 reduce_window_sum.11
  4.1 0.1 select_reduce_fusion.1
  4.3 14.3 %all_to_all.19 = s32[32,1,2]{2,1,0:T(1,128)S(1)} all-to-all(s32[32,1,2]{2,1,0:T(1,128)S(1)} %copy.31), channel_id=1, replica_groups=mesh['rows'=8,'grp'=4] {'rows','grp'}, dimensions={0} | all-to-all | bytes 512 | tf_op jit(solution)/shard_map/all_to_all | solution.py:34
  18.6 0.5 broadcast.327
  19.2 0.7 fusion.14
  19.9 0.1 reshape.184
  20.0 2.7 gather_fusion.1
  22.8 3.6 all-to-all-start.1
  26.4 1.3 gather_fusion.2
  27.7 93.0 %all-to-all-done.1 = bf16[32,2,128,256]{3,2,1,0:T(8,128)(2,1)} async-done(((bf16[32,2,128,256]{3,2,1,0:T(8,128)(2,1)}), bf16[32,2,128,256]{3,2,1,0:T(8,128)(2,1)}, u32[]{:S(2)}, u32[]{:S(2)}) %all-to-all-start.1) | async-done | bytes 4194336 | tf_op jit(solution)/shard_map/all_to_all | solution.py:36
  120.8 8.8 %gather_fusion.3 = bf16[128,128,256]{2,1,0:T(8,128)(2,1)} fusion(bf16[64,128,256]{2,1,0:T(8,128)(2,1)} %bitcast.5, s32[1024]{0:T(1024)S(1)} %pad_clamp_fusion.1), kind=kCustom, calls=%fused_computation.3 | custom fusion | bytes 16777728 | tf_op jit(solution)/shard_map/gather | solution.py:39
  129.5 12.7 %convolution_bitcast_fusion.1 = f32[128,128,256]{1,2,0:T(8,128)} fusion(bf16[128,128,256]{2,1,0:T(8,128)(2,1)} %gather_fusion.3, bf16[128,128,128]{2,1,0:T(8,128)(2,1)} %param.6), kind=kOutput, calls=%fused_computation.8 | convolution fusion | flops 1073741824 | bytes 29360128 | tf_op jit(solution)/shard_map/tij,tjk->tik/dot_general | solution.py:40
  142.2 17.5 %copy.33 = f32[128,128,256]{2,1,0:T(8,128)} copy(f32[128,128,256]{1,2,0:T(8,128)} %convolution_bitcast_fusion.1) | data formatting | bytes 33554432 | tf_op jit(solution)/shard_map/tij,tjk->tik/dot_general | solution.py:40
  159.6 3.4 broadcast_in_dim.40
  163.1 37.4 %scatter_fusion = f32[48,128,256]{2,1,0:T(8,128)} fusion(f32[48,128,256]{2,1,0:T(8,128)} %broadcast_in_dim.40, s32[128]{0:T(128)S(1)} %get-tuple-element.18, f32[128,128,256]{2,1,0:T(8,128)} %copy.33), kind=kCustom, calls=%fused_computation.5 | custom fusion | flops 4194304 | bytes 50332160 | tf_op jit(solution)/shard_map/scatter-add | solution.py:42
  200.4 4.9 %convert_element_type.11 = bf16[48,128,256]{2,1,0:T(8,128)(2,1)} convert(f32[48,128,256]{2,1,0:T(8,128)} %scatter_fusion) | non-fusion elementwise | flops 1572864 | bytes 9437184 | tf_op jit(solution)/shard_map/convert_element_type | solution.py:42
  205.3 8.5 %gather_fusion.4 = bf16[128,128,256]{2,1,0:T(8,128)(2,1)} fusion(bf16[48,128,256]{2,1,0:T(8,128)(2,1)} %convert_element_type.11, s32[1024]{0:T(1024)S(1)} %pad_clamp_fusion), kind=kCustom, calls=%fused_computation.4 | custom fusion | bytes 16777728 | tf_op jit(solution)/shard_map/gather | solution.py:44
  213.8 12.7 %convolution_bitcast_fusion = f32[128,128,256]{1,2,0:T(8,128)} fusion(bf16[128,128,256]{2,1,0:T(8,128)(2,1)} %gather_fusion.4, bf16[128,128,128]{2,1,0:T(8,128)(2,1)} %param.6), kind=kOutput, calls=%fused_computation.7 | convolution fusion | flops 1073741824 | bytes 29360128 | tf_op jit(solution)/shard_map/tij,tik->tjk/dot_general | solution.py:43
  226.5 17.5 %copy.35 = f32[128,128,256]{2,1,0:T(8,128)} copy(f32[128,128,256]{1,2,0:T(8,128)} %convolution_bitcast_fusion) | data formatting | bytes 33554432 | tf_op jit(solution)/shard_map/tij,tik->tjk/dot_general | solution.py:43
  243.9 4.2 %broadcast_in_dim.46 = f32[64,128,256]{2,1,0:T(8,128)} broadcast(f32[]{:T(128)} %constant.20.clone.1), dimensions={} | broadcast | bytes 8388612 | tf_op jit(solution)/shard_map/broadcast_in_dim | solution.py:47
  248.2 36.7 %scatter_fusion.1 = f32[64,128,256]{2,1,0:T(8,128)} fusion(f32[64,128,256]{2,1,0:T(8,128)} %broadcast_in_dim.46, s32[128]{0:T(128)S(1)} %get-tuple-element.15, f32[128,128,256]{2,1,0:T(8,128)} %copy.35), kind=kCustom, calls=%fused_computation.6 | custom fusion | flops 4194304 | bytes 50332160 | tf_op jit(solution)/shard_map/scatter-add | solution.py:47
  284.9 4.0 convert_element_type.12
  288.9 6.4 %copy.36 = bf16[32,2,128,256]{3,1,2,0:T(2,128)(2,1)} copy(bf16[32,2,128,256]{3,2,1,0:T(8,128)(2,1)S(1)} %bitcast.62) | data formatting | bytes 8388608 | tf_op jit(solution)/shard_map/reshape | solution.py:50
  295.3 5.8 %all-to-all-start.2 = ((bf16[32,2,128,256]{3,1,2,0:T(2,128)(2,1)}), bf16[32,2,128,256]{3,1,2,0:T(2,128)(2,1)}, u32[]{:S(2)}, u32[]{:S(2)}) async-start(bf16[32,2,128,256]{3,1,2,0:T(2,128)(2,1)} %copy.36), calls=%async_computation.2 | async-start | bytes 8388608 | tf_op jit(solution)/shard_map/all_to_all | solution.py:51
  301.2 94.1 %all-to-all-done.2 = bf16[32,2,128,256]{3,1,2,0:T(2,128)(2,1)} async-done(((bf16[32,2,128,256]{3,1,2,0:T(2,128)(2,1)}), bf16[32,2,128,256]{3,1,2,0:T(2,128)(2,1)}, u32[]{:S(2)}, u32[]{:S(2)}) %all-to-all-start.2) | async-done | bytes 4194336 | tf_op jit(solution)/shard_map/all_to_all | solution.py:51
  395.3 9.0 %copy.37 = bf16[32,2,128,256]{3,1,0,2:T(2,128)(2,1)} copy(bf16[32,2,128,256]{3,1,2,0:T(2,128)(2,1)} %all-to-all-done.2) | data formatting | bytes 8388608 | tf_op jit(solution)/shard_map/all_to_all | solution.py:51
  404.3 7.2 %reshape.173 = bf16[64,128,256]{2,0,1:T(8,128)(2,1)} reshape(bf16[32,2,128,256]{3,1,0,2:T(2,128)(2,1)} %copy.37) | data formatting | bytes 8388608 | tf_op jit(solution)/shard_map/reshape | solution.py:52
  411.5 2.9 fusion.3
  414.3 2.5 copy.38
  (19 shorter events, 0.4 us)
Async XLA Ops:
  0.6 19.4 %copy-start = (bf16[16,128,256]{2,1,0:T(8,128)(2,1)S(1)}, bf16[16,128,256]{2,1,0:T(8,128)(2,1)}, u32[]{:S(2)}) copy-start(bf16[16,128,256]{2,1,0:T(8,128)(2,1)} %param.11) | copy-start | bytes 3145732
  20.0 7.7 %copy-start.2 = (s32[128]{0:T(128)S(1)}, s32[128]{0:T(128)}, u32[]{:S(2)}) copy-start(s32[128]{0:T(128)} %param.7) | copy-start | bytes 1540
  22.8 98.0 %all-to-all-start.1 = ((bf16[32,2,128,256]{3,2,1,0:T(8,128)(2,1)}), bf16[32,2,128,256]{3,2,1,0:T(8,128)(2,1)}, u32[]{:S(2)}, u32[]{:S(2)}) async-start(bf16[32,2,128,256]{3,2,1,0:T(8,128)(2,1)} %bitcast.63), calls=%async_computation.1 | async-start | bytes 8388608 | tf_op jit(solution)/shard_map/all_to_all | solution.py:36
  295.3 100.0 %all-to-all-start.2 = ((bf16[32,2,128,256]{3,1,2,0:T(2,128)(2,1)}), bf16[32,2,128,256]{3,1,2,0:T(2,128)(2,1)}, u32[]{:S(2)}, u32[]{:S(2)}) async-start(bf16[32,2,128,256]{3,1,2,0:T(2,128)(2,1)} %copy.36), calls=%async_computation.2 | async-start | bytes 8388608 | tf_op jit(solution)/shard_map/all_to_all | solution.py:51
  395.3 21.6 %copy-start.1 = (bf16[16,128,256]{2,1,0:T(8,128)(2,1)S(1)}, bf16[16,128,256]{2,1,0:T(8,128)(2,1)}, u32[]{:S(2)}) copy-start(bf16[16,128,256]{2,1,0:T(8,128)(2,1)} %param.11) | copy-start | bytes 3145732
where the time goes:
time: 418 us; the launch traced here: 417 us
  waiting for transfers between devices  187 us (45%)
  local copies, waits for them, and re-layouts  91.5 us (22%)
  other arithmetic  85 us (20%)
  matrix products  28.2 us (7%)
  blocking collectives  14.3 us (3%)
  starting transfers between devices  9.36 us (2%)
    all_to_all x1, waiting for transfers between devices, per_device(): lax.all_to_all(outbound, ('rows', 'grp'), split_axis=0, concat_axis=0, ti...  94.1 us
    all_to_all x1, waiting for transfers between devices, per_device(): lax.all_to_all(outgoing, ('rows', 'grp'), split_axis=0, concat_axis=0, ti...  93 us
    scatter-add x1, other arithmetic, per_device(): jax.ops.segment_sum(product, row_ids, num_segments=RB_DEV)  37.4 us
    scatter-add x1, other arithmetic, per_device(): jax.ops.segment_sum(partial_value, slot_rows, num_segments=devices * PAIR...  36.7 us
    dot_general x1, local copies, waits for them, and re-layouts, per_device(): jnp.einsum('tij,tjk->tik', tiles, per_tile, preferred_element_type=jnp.fl...  17.5 us
    dot_general x1, local copies, waits for them, and re-layouts, per_device(): jnp.einsum('tij,tik->tjk', tiles, sketch[tile_rows], preferred_element_ty...  17.5 us
    all_to_all x1, blocking collectives, per_device(): lax.all_to_all(wanted, ('rows', 'grp'), split_axis=0, concat_axis=0, tile...  14.3 us
    dot_general x1, matrix products, per_device(): jnp.einsum('tij,tjk->tik', tiles, per_tile, preferred_element_type=jnp.fl...  12.7 us
  transfers between devices with their start and end apart: 2, of which 2 were waited for; matrix products, arithmetic and copies ran while one was open for 0% of the time, Pallas kernels for 0%

commit v1 on v0

v1 whole, which is shorter than its diff:
```python
import functools

import jax
import jax.numpy as jnp
from jax import lax
from jax.experimental import pallas as pl
from jax.experimental.pallas import tpu as pltpu
from jax.sharding import PartitionSpec as P

RB_DEV = 48
PAIR_CAP = 2
UNROLL = 4
AXES = ("rows", "grp")
VMEM_LIMIT = 60 * 1024 * 1024


def index_tables(tile_rows, tile_cols, tile_count, block_perm, devices, held):
    slots = tile_cols.shape[0]
    live = jnp.arange(slots, dtype=jnp.int32) < tile_count[0]
    blocks = jnp.arange(block_perm.shape[0], dtype=jnp.int32)
    stored = jnp.sum(jnp.where(tile_cols[:, None] == blocks[None, :], block_perm[None, :], 0), axis=1)
    owner = stored // held
    local = stored % held
    rank = jnp.any(
        live[None, :] & (owner[None, :] == owner[:, None]) & (local[None, :] < local[:, None]), axis=1
    ).astype(jnp.int32)
    mine = live[None, :] & (owner[None, :] == jnp.arange(devices, dtype=jnp.int32)[:, None])
    first = jnp.min(jnp.where(mine, local[None, :], held), axis=1)
    last = jnp.max(jnp.where(mine, local[None, :], -1), axis=1)
    wanted = jnp.stack(
        [jnp.where(last >= 0, first, -1), jnp.where(last > first, last, -1)], axis=-1
    ).astype(jnp.int32)
    slot = jnp.where(live, owner * PAIR_CAP + rank, devices * PAIR_CAP)
    row = jnp.where(live, tile_rows, RB_DEV)
    return wanted, slot.astype(jnp.int32), row.astype(jnp.int32)


def pick_kernel(asked, panel, out):
    def body(j, c):
        out[j] = panel[jnp.maximum(asked[j], 0)]
        return c

    lax.fori_loop(0, out.shape[0], body, 0, unroll=4)


def product_kernel(count, slot, row, tiles, fetched, sketch, outbound, sk, part):
    nslots = outbound.shape[0]
    steps = (count[0] + UNROLL - 1) // UNROLL

    def clear(ref):
        def body(i, c):
            ref[i] = jnp.zeros(ref.shape[1:], ref.dtype)
            return c

        lax.fori_loop(0, ref.shape[0], body, 0)

    clear(sk)
    clear(part)

    def forward(i, c):
        got = []
        for u in range(UNROLL):
            t = i * UNROLL + u
            block = fetched[jnp.minimum(slot[t], nslots - 1)]
            got.append(jnp.dot(tiles[t], block, preferred_element_type=jnp.float32))
        for u in range(UNROLL):
            r = row[i * UNROLL + u]
            sk[r] = sk[r] + got[u]
        return c

    lax.fori_loop(0, steps, forward, 0)

    def rounded(i, c):
        sketch[i] = sk[i].astype(sketch.dtype)
        return c

    lax.fori_loop(0, sketch.shape[0], rounded, 0)

    def backward(i, c):
        got = []
        for u in range(UNROLL):
            t = i * UNROLL + u
            block = sketch[jnp.minimum(row[t], sketch.shape[0] - 1)]
            got.append(
                lax.dot_general(
                    tiles[t], block, (((0,), (0,)), ((), ())), preferred_element_type=jnp.float32
                )
            )
        for u in range(UNROLL):
            s = slot[i * UNROLL + u]
            part[s] = part[s] + got[u]
        return c

    lax.fori_loop(0, steps, backward, 0)

    def send_form(i, c):
        outbound[i] = part[i].astype(outbound.dtype)
        return c

    lax.fori_loop(0, nslots, send_form, 0)


def gram_kernel(asked, inbound, gram):
    def clear(i, c):
        gram[i] = jnp.zeros(gram.shape[1:], gram.dtype)
        return c

    lax.fori_loop(0, gram.shape[0], clear, 0)

    def body(j, c):
        b = asked[j]

        @pl.when(b >= 0)
        def _():
            gram[b] = gram[b] + inbound[j].astype(jnp.float32)

        return c

    lax.fori_loop(0, inbound.shape[0], body, 0)


SMEM = pl.BlockSpec(memory_space=pltpu.SMEM)
VMEM = pl.BlockSpec(memory_space=pltpu.VMEM)


def per_device(tiles, tile_rows, tile_cols, tile_count, block_perm, panel):
    devices = lax.axis_size(AXES)
    held, depth, width = panel.shape
    nslots = devices * PAIR_CAP
    part = width if nslots <= tiles.shape[0] else width // 2
    wanted, slot, row = index_tables(tile_rows, tile_cols, tile_count, block_perm, devices, held)
    asked = lax.all_to_all(wanted, AXES, split_axis=0, concat_axis=0, tiled=True).reshape(-1)
    params = pltpu.CompilerParams(vmem_limit_bytes=VMEM_LIMIT)
    outgoing = pl.pallas_call(
        pick_kernel,
        out_shape=jax.ShapeDtypeStruct((nslots, depth, width), panel.dtype),
        in_specs=[SMEM, VMEM],
        out_specs=VMEM,
        compiler_params=params,
    )(asked, panel)
    fetched = lax.all_to_all(outgoing, AXES, split_axis=0, concat_axis=0, tiled=True)
    sketch, outbound = pl.pallas_call(
        product_kernel,
        out_shape=(
            jax.ShapeDtypeStruct((RB_DEV, depth, width), jnp.bfloat16),
            jax.ShapeDtypeStruct((nslots, depth, width), jnp.bfloat16),
        ),
        grid=(width // part,),
        in_specs=[
            SMEM,
            SMEM,
            SMEM,
            pl.BlockSpec(tiles.shape, lambda k: (0, 0, 0), pipeline_mode=pl.Buffered(1)),
            pl.BlockSpec((nslots, depth, part), lambda k: (0, 0, k), pipeline_mode=pl.Buffered(1)),
        ],
        out_specs=(
            pl.BlockSpec((RB_DEV, depth, part), lambda k: (0, 0, k), pipeline_mode=pl.Buffered(1)),
            pl.BlockSpec((nslots, depth, part), lambda k: (0, 0, k), pipeline_mode=pl.Buffered(1)),
        ),
        scratch_shapes=[
            pltpu.VMEM((RB_DEV + 1, depth, part), jnp.float32),
            pltpu.VMEM((nslots + 1, depth, part), jnp.float32),
        ],
        compiler_params=params,
    )(tile_count, slot, row, tiles, fetched.reshape(nslots, depth, width))
    inbound = lax.all_to_all(outbound, AXES, split_axis=0, concat_axis=0, tiled=True)
    gram = pl.pallas_call(
        gram_kernel,
        out_shape=jax.ShapeDtypeStruct((held, depth, width), jnp.float32),
        in_specs=[SMEM, VMEM],
        out_specs=VMEM,
        compiler_params=params,
    )(asked, inbound.reshape(nslots, depth, width))
    return sketch, gram


def solution(mesh):
    spec = P(AXES, None, None)
    return jax.shard_map(
        per_device,
        mesh=mesh,
        in_specs=(spec, P(AXES), P(AXES), P(AXES), P(), spec),
        out_specs=(spec, spec),
        check_vma=False,
    )
```

time: 418 us -> 247 us (0.59)
  blocking collectives: 14.3 us -> 122 us
  waiting for transfers between devices: 187 us -> 93.7 us
  local copies, waits for them, and re-layouts: 91.5 us -> 1.19 us
  other arithmetic: 85 us -> 2.41 us
  matrix products: 28.2 us -> 0 us
  Pallas kernels: 0 us -> 22.9 us
  starting transfers between devices: 9.36 us -> 3.7 us
    all_to_all x1 -> x2, blocking collectives: 14.3 us -> 122 us  [the longest x1 108 us: per_device(): lax.all_to_all(outbound, AXES, split_axis=0, concat_axis=0, tiled=True)]
    all_to_all x2 -> x1, waiting for transfers between devices: 187 us -> 93.7 us  [per_device(): lax.all_to_all(outgoing, AXES, split_axis=0, concat_axis=0, tiled=True)]
    scatter-add x2 -> x0, other arithmetic: 74.1 us -> none  [the longest x1 37.4 us: per_device(): jax.ops.segment_sum(product, row_ids, num_segments=RB_DEV)]
    dot_general x2 -> x0, local copies, waits for them, and re-layouts: 34.9 us -> none  [the longest x1 17.5 us: per_device(): jnp.einsum('tij,tjk->tik', tiles, per_tile, preferred_element_type=jnp.fl...]
    dot_general x3 -> x0, matrix products: 28.2 us -> none  [the longest x1 12.7 us: per_device(): jnp.einsum('tij,tjk->tik', tiles, per_tile, preferred_element_type=jnp.fl...]
    pallas_call x0 -> x3, Pallas kernels: none -> 22.9 us  [the longest x1 14.3 us: per_device(): pl.pallas_call(product_kernel, out_shape=(jax.ShapeDtypeStruct((RB_DEV, d...]
    gather x5 -> x0, local copies, waits for them, and re-layouts: 22.9 us -> none  [the longest x1 8.75 us: per_device(): fetched.reshape((devices * PAIR_CAP,) + fetched.shape[2:])[slot_of]]
    reshape x3 -> x1, local copies, waits for them, and re-layouts: 13.7 us -> 0.59 us  [per_device(): lax.all_to_all(wanted, AXES, split_axis=0, concat_axis=0, tiled=True)]
  transfers between devices with their start and end apart: 2 -> 1, of which waited for: 2 -> 1; matrix products, arithmetic and copies ran while one was open for 0% -> 0% of each run, Pallas kernels for 0% -> 0%
where the time goes in v1:
time: 247 us
  blocking collectives  122 us (49%)
  waiting for transfers between devices  93.7 us (38%)
  Pallas kernels  22.9 us (9%)
  starting transfers between devices  3.7 us (1%)
    all_to_all x1, blocking collectives, per_device(): lax.all_to_all(outbound, AXES, split_axis=0, concat_axis=0, tiled=True)  108 us
    all_to_all x1, waiting for transfers between devices, per_device(): lax.all_to_all(outgoing, AXES, split_axis=0, concat_axis=0, tiled=True)  93.7 us
    all_to_all x1, blocking collectives, per_device(): lax.all_to_all(wanted, AXES, split_axis=0, concat_axis=0, tiled=True)  14.3 us
    pallas_call x1, Pallas kernels, per_device(): pl.pallas_call(product_kernel, out_shape=(jax.ShapeDtypeStruct((RB_DEV, d...  14.3 us
    pallas_call x1, Pallas kernels, per_device(): pl.pallas_call(gram_kernel, out_shape=jax.ShapeDtypeStruct((held, depth,...  5.06 us
  transfers between devices with their start and end apart: 1, of which 1 were waited for; matrix products, arithmetic and copies ran while one was open for 0% of the time, Pallas kernels for 0%

profile of v1, /device:TPU:0, one launch (start us, length us, event | category | flops | bytes accessed | tf_op | source)
XLA Modules:
  0.0 247.1 jit_solution(10974620412071152466)
XLA Ops:
  1.3 0.9 select_reduce_fusion
  2.2 0.1 select_reduce_fusion.2
  2.3 0.1 copy.11
  2.4 14.3 %all_to_all.19 = s32[32,1,2]{2,1,0:T(1,128)S(1)} all-to-all(s32[32,1,2]{2,1,0:T(1,128)S(1)} %copy.11), channel_id=1, replica_groups=mesh['rows'=8,'grp'=4] {'rows','grp'}, dimensions={0} | all-to-all | bytes 512 | tf_op jit(solution)/shard_map/all_to_all | solution.py:132
  16.7 0.5 broadcast.144
  17.2 0.7 reduce.3
  17.9 0.6 reshape.104.asked
  18.5 3.6 %shard_map.77 = bf16[64,128,256]{2,1,0:T(8,128)(2,1)} custom-call(s32[64]{0:T(128)} %reshape.104.asked, bf16[16,128,256]{2,1,0:T(8,128)(2,1)} %panel.1), custom_call_target="tpu_custom_call" | custom-call | tf_op jit(solution)/shard_map/pallas_call | solution.py:134
  22.1 0.0 copy-start
  22.1 3.7 %all-to-all-start.1 = ((bf16[64,128,256]{2,1,0:T(8,128)(2,1)}), bf16[64,128,256]{2,1,0:T(8,128)(2,1)}, u32[]{:S(2)}, u32[]{:S(2)}) async-start(bf16[64,128,256]{2,1,0:T(8,128)(2,1)} %shard_map.77), calls=%async_computation.1 | async-start | bytes 8388608 | tf_op jit(solution)/shard_map/all_to_all | solution.py:141
  25.8 0.2 and_reduce_fusion
  26.0 0.0 copy-done
  26.0 0.5 add_select_fusion
  26.5 93.7 %all-to-all-done.1.fetched = bf16[64,128,256]{2,1,0:T(8,128)(2,1)} async-done(((bf16[64,128,256]{2,1,0:T(8,128)(2,1)}), bf16[64,128,256]{2,1,0:T(8,128)(2,1)}, u32[]{:S(2)}, u32[]{:S(2)}) %all-to-all-start.1) | async-done | bytes 4194336 | tf_op jit(solution)/shard_map/all_to_all | solution.py:141
  120.2 14.3 %shard_map.78 = (bf16[48,128,256]{2,1,0:T(8,128)(2,1)}, bf16[64,128,256]{2,1,0:T(8,128)(2,1)}) custom-call(s32[1]{0:T(128)} %copy.12.count, s32[128]{0:T(128)} %get-tuple-element.12.slot, s32[128]{0:T(128)} %get-tuple-element.13.row, bf16[128,128,128]{2,1,0:T(8,128)(2,1)} %tiles.1, bf16[64,128,256]{2,1,0:T(8,128)(2,1)} %all-to-all-done.1.fetched), custom_call_target="tpu_custom_call" | custom-call | tf_op jit(solution)/shard_map/pallas_call | solution.py:142
  134.4 107.6 %all_to_all.20.inbound = bf16[64,128,256]{2,1,0:T(8,128)(2,1)} all-to-all(bf16[64,128,256]{2,1,0:T(8,128)(2,1)} %get-tuple-element.5), channel_id=1, replica_groups=mesh['rows'=8,'grp'=4] {'rows','grp'}, dimensions={0} | all-to-all | bytes 8388608 | tf_op jit(solution)/shard_map/all_to_all | solution.py:166
  242.1 5.1 %shard_map.79 = f32[16,128,256]{2,1,0:T(8,128)} custom-call(s32[64]{0:T(128)} %reshape.104.asked, bf16[64,128,256]{2,1,0:T(8,128)(2,1)} %all_to_all.20.inbound), custom_call_target="tpu_custom_call" | custom-call | tf_op jit(solution)/shard_map/pallas_call | solution.py:167
  (4 shorter events, 0.0 us)
Async XLA Ops:
  22.1 3.9 %copy-start = (s32[128]{0:T(128)S(1)}, s32[128]{0:T(128)}, u32[]{:S(2)}) copy-start(s32[128]{0:T(128)} %param.7) | copy-start | bytes 1540
  22.1 98.1 %all-to-all-start.1 = ((bf16[64,128,256]{2,1,0:T(8,128)(2,1)}), bf16[64,128,256]{2,1,0:T(8,128)(2,1)}, u32[]{:S(2)}, u32[]{:S(2)}) async-start(bf16[64,128,256]{2,1,0:T(8,128)(2,1)} %shard_map.77), calls=%async_computation.1 | async-start | bytes 8388608 | tf_op jit(solution)/shard_map/all_to_all | solution.py:141

commit v2 on v1

--- a/solution.py
+++ b/solution.py
@@ -35,12 +35,144 @@
     return wanted, slot.astype(jnp.int32), row.astype(jnp.int32)
 
 
-def pick_kernel(asked, panel, out):
-    def body(j, c):
-        out[j] = panel[jnp.maximum(asked[j], 0)]
-        return c
-
-    lax.fori_loop(0, out.shape[0], body, 0, unroll=4)
+LINE = 4
+MESH = pl.DeviceIdType.MESH
+
+
+class Place:
+    def __init__(self, line, rows, grp):
+        self.line, self.grp = line, grp
+        self.plane_rows = rows // line
+        self.plane = self.plane_rows * grp
+        row = lax.axis_index("rows")
+        self.z = row // self.plane_rows
+        self.p = (row % self.plane_rows) * grp + lax.axis_index("grp")
+
+    def device(self, z, p):
+        return (z * self.plane_rows + p // self.grp, p % self.grp)
+
+    def peer(self, i):
+        return lax.rem(self.p + i, self.plane)
+
+    def greet(self):
+        barrier = pltpu.get_barrier_semaphore()
+        for k in range(1, self.line):
+            to = self.device(lax.rem(self.z + k, self.line), self.p)
+            pl.semaphore_signal(barrier, inc=1, device_id=to, device_id_type=MESH)
+
+        def signal(i, c):
+            to = self.device(self.z, self.peer(i))
+            pl.semaphore_signal(barrier, inc=1, device_id=to, device_id_type=MESH)
+            return c
+
+        lax.fori_loop(1, self.plane, signal, 0)
+        pl.semaphore_wait(barrier, self.line - 1 + self.plane - 1)
+
+    def inside(self, z):
+        return (z >= 0) & (z < self.line)
+
+
+def remote(src, dst, send, recv, to):
+    return pltpu.make_async_remote_copy(
+        src_ref=src, dst_ref=dst, send_sem=send, recv_sem=recv, device_id=to, device_id_type=MESH
+    )
+
+
+def fetch_kernel(line, rows, grp, wanted, panel, fetched, asked, *scratch):
+    far, (ids, out, id_send, id_recv, z_send, z_recv, send, recv, local) = (
+        scratch[: 2 * (line - 1)],
+        scratch[2 * (line - 1) :],
+    )
+    at = Place(line, rows, grp)
+    z, p, plane = at.z, at.p, at.plane
+    at.greet()
+
+    def unit(way, k):
+        return panel if k == 0 else far[way * (line - 1) + k - 1]
+
+    def along(way, k):
+        step = 1 if way == 0 else -1
+        to = at.device(jnp.clip(z + step, 0, line - 1), p)
+        return remote(unit(way, k - 1), unit(way, k), z_send.at[way, k - 1], z_recv.at[way, k - 1], to)
+
+    def source(way, k):
+        return z - k if way == 0 else z + k
+
+    def sends(way, k):
+        return at.inside(z + (1 if way == 0 else -1)) & at.inside(source(way, k - 1))
+
+    def id_copy(i, mine):
+        q = at.peer(i)
+        slot = p if mine else q
+        return remote(wanted.at[q], asked.at[slot], id_send.at[q], id_recv.at[slot], at.device(z, q))
+
+    def start_ids(i, c):
+        id_copy(i, True).start()
+        return c
+
+    lax.fori_loop(1, plane, start_ids, 0)
+    for way in range(2):
+        pl.when(sends(way, 1))(lambda way=way: along(way, 1).start())
+    asked[p] = wanted[p]
+
+    def wait_ids(i, c):
+        id_copy(i, False).wait()
+        return c
+
+    lax.fori_loop(1, plane, wait_ids, 0)
+    to_smem = pltpu.make_async_copy(asked, ids, local)
+    to_smem.start()
+    to_smem.wait()
+
+    def spread(plane_z, held):
+        def pick(i, c):
+            q = at.peer(i)
+            for j in range(PAIR_CAP):
+                block = jnp.maximum(ids[q, 0, plane_z * PAIR_CAP + j], 0)
+                out[plane_z, q, j] = held[block]
+            return c
+
+        lax.fori_loop(1, plane, pick, 0)
+        for j in range(PAIR_CAP):
+            block = jnp.maximum(ids[p, 0, plane_z * PAIR_CAP + j], 0)
+            fetched[plane_z, p, j] = held[block]
+
+        def start(i, c):
+            q = at.peer(i)
+            remote(
+                out.at[plane_z, q], fetched.at[plane_z, p], send.at[plane_z, q], recv.at[plane_z, p], at.device(z, q)
+            ).start()
+            return c
+
+        lax.fori_loop(1, plane, start, 0)
+
+    spread(z, panel)
+    for k in range(1, line):
+        for way in range(2):
+
+            def pass_on(way=way, k=k):
+                along(way, k).wait_recv()
+                if k + 1 < line:
+                    pl.when(sends(way, k + 1))(lambda: along(way, k + 1).start())
+
+            pl.when(at.inside(source(way, k)))(pass_on)
+        for way in range(2):
+            pl.when(at.inside(source(way, k)))(
+                lambda way=way, k=k: spread(source(way, k), unit(way, k))
+            )
+    for k in range(1, line):
+        for way in range(2):
+            pl.when(sends(way, k))(lambda way=way, k=k: along(way, k).wait_send())
+
+    def finish(i, c):
+        q = at.peer(i)
+        for plane_z in range(line):
+            remote(
+                out.at[plane_z, q], fetched.at[plane_z, q], send.at[plane_z, q], recv.at[plane_z, q], at.device(z, q)
+            ).wait()
+        return c
+
+    lax.fori_loop(1, plane, finish, 0)
 
 
 def product_kernel(count, slot, row, tiles, fetched, sketch, outbound, sk, part):
@@ -100,45 +232,155 @@
     lax.fori_loop(0, nslots, send_form, 0)
 
 
-def gram_kernel(asked, inbound, gram):
-    def clear(i, c):
-        gram[i] = jnp.zeros(gram.shape[1:], gram.dtype)
-        return c
-
-    lax.fori_loop(0, gram.shape[0], clear, 0)
-
-    def body(j, c):
-        b = asked[j]
-
-        @pl.when(b >= 0)
-        def _():
-            gram[b] = gram[b] + inbound[j].astype(jnp.float32)
-
-        return c
-
-    lax.fori_loop(0, inbound.shape[0], body, 0)
+def reduce_kernel(line, rows, grp, ids, outbound, gram, inb, came, gone, total, z_send, z_recv, send, recv):
+    at = Place(line, rows, grp)
+    z, p, plane = at.z, at.p, at.plane
+    held = gram.shape[0]
+    at.greet()
+
+    def target(way, k):
+        return z + k if way == 0 else z - k
+
+    def along(way, k):
+        to = at.device(jnp.clip(target(way, 1), 0, line - 1), p)
+        return remote(
+            gone.at[way, k - 1], came.at[way, k - 1], z_send.at[way, k - 1], z_recv.at[way, k - 1], to
+        )
+
+    def begin(plane_z):
+        def start(i, c):
+            q = at.peer(i)
+            remote(
+                outbound.at[plane_z, q], inb.at[plane_z, p], send.at[plane_z, q], recv.at[plane_z, p], at.device(z, q)
+            ).start()
+            return c
+
+        lax.fori_loop(1, plane, start, 0)
+        for j in range(PAIR_CAP):
+            inb[plane_z, p, j] = outbound[plane_z, p, j]
+
+    def add_up(plane_z, into):
+        def arrive(i, c):
+            q = at.peer(i)
+            remote(
+                outbound.at[plane_z, q], inb.at[plane_z, q], send.at[plane_z, q], recv.at[plane_z, q], at.device(z, q)
+            ).wait()
+            return c
+
+        lax.fori_loop(1, plane, arrive, 0)
+
+        def block(b, c):
+            def term(q, acc):
+                for j in range(PAIR_CAP):
+                    hit = ids[q, 0, plane_z * PAIR_CAP + j] == b
+                    acc = acc + jnp.where(hit, inb[plane_z, q, j].astype(jnp.float32), 0.0)
+                return acc
+
+            zero = jnp.zeros(into.shape[1:], jnp.float32)
+            into[b] = lax.fori_loop(0, plane, term, zero, unroll=8)
+            return c
+
+        lax.fori_loop(0, held, block, 0)
+
+    stages = [(way, k) for k in range(line - 1, 0, -1) for way in range(2)]
+    for way, k in stages:
+        pl.when(at.inside(target(way, k)))(lambda way=way, k=k: begin(target(way, k)))
+    begin(z)
+    for k in range(line - 1, 0, -1):
+        for way in range(2):
+            pl.when(at.inside(target(way, k)))(
+                lambda way=way, k=k: add_up(target(way, k), total.at[way])
+            )
+        for way in range(2):
+            has = at.inside(target(way, -1))
+
+            def joined(way=way, k=k):
+                along(way, k + 1).wait_recv()
+
+                def block(b, c):
+                    gone[way, k - 1, b] = (
+                        total[way, b] + came[way, k, b].astype(jnp.float32)
+                    ).astype(gone.dtype)
+                    return c
+
+                lax.fori_loop(0, held, block, 0)
+
+            def alone(way=way, k=k):
+                def block(b, c):
+                    gone[way, k - 1, b] = total[way, b].astype(gone.dtype)
+                    return c
+
+                lax.fori_loop(0, held, block, 0)
+
+            def stage(way=way, k=k, has=has, joined=joined, alone=alone):
+                if k + 1 < line:
+                    pl.when(has)(joined)
+                    pl.when(jnp.logical_not(has))(alone)
+                else:
+                    alone()
+                along(way, k).start()
+
+            pl.when(at.inside(target(way, k)))(stage)
+    add_up(z, gram)
+    for way in range(2):
+
+        def last(way=way):
+            along(way, 1).wait_recv()
+
+            def block(b, c):
+                gram[b] = gram[b] + came[way, 0, b].astype(jnp.float32)
+                return c
+
+            lax.fori_loop(0, held, block, 0)
+
+        pl.when(at.inside(target(way, -1)))(last)
+    for way, k in stages:
+        pl.when(at.inside(target(way, k)))(lambda way=way, k=k: along(way, k).wait_send())
 
 
 SMEM = pl.BlockSpec(memory_space=pltpu.SMEM)
 VMEM = pl.BlockSpec(memory_space=pltpu.VMEM)
+DMA = pltpu.SemaphoreType.DMA
 
 
 def per_device(tiles, tile_rows, tile_cols, tile_count, block_perm, panel):
-    devices = lax.axis_size(AXES)
+    rows, grp = lax.axis_size("rows"), lax.axis_size("grp")
+    devices = rows * grp
+    line = LINE if rows % LINE == 0 else rows
+    plane = devices // line
     held, depth, width = panel.shape
     nslots = devices * PAIR_CAP
     part = width if nslots <= tiles.shape[0] else width // 2
     wanted, slot, row = index_tables(tile_rows, tile_cols, tile_count, block_perm, devices, held)
-    asked = lax.all_to_all(wanted, AXES, split_axis=0, concat_axis=0, tiled=True).reshape(-1)
+    by_peer = wanted.reshape(line, plane, PAIR_CAP).transpose(1, 0, 2).reshape(plane, 1, line * PAIR_CAP)
+    by_peer = jnp.pad(by_peer, ((0, 0), (0, 7), (0, 128 - line * PAIR_CAP)))
+    paired = (line, plane, PAIR_CAP, depth, width)
+    unit = pltpu.VMEM(panel.shape, panel.dtype)
     params = pltpu.CompilerParams(vmem_limit_bytes=VMEM_LIMIT)
-    outgoing = pl.pallas_call(
-        pick_kernel,
-        out_shape=jax.ShapeDtypeStruct((nslots, depth, width), panel.dtype),
-        in_specs=[SMEM, VMEM],
-        out_specs=VMEM,
-        compiler_params=params,
-    )(asked, panel)
-    fetched = lax.all_to_all(outgoing, AXES, split_axis=0, concat_axis=0, tiled=True)
+    fetched, asked = pl.pallas_call(
+        functools.partial(fetch_kernel, line, rows, grp),
+        out_shape=(
+            jax.ShapeDtypeStruct(paired, panel.dtype),
+            jax.ShapeDtypeStruct(by_peer.shape, jnp.int32),
+        ),
+        in_specs=[VMEM, VMEM],
+        out_specs=(VMEM, VMEM),
+        scratch_shapes=[unit] * (2 * (line - 1))
+        + [
+            pltpu.SMEM(by_peer.shape, jnp.int32),
+            pltpu.VMEM(paired, panel.dtype),
+            DMA((plane,)),
+            DMA((plane,)),
+            DMA((2, line - 1)),
+            DMA((2, line - 1)),
+            DMA((line, plane)),
+            DMA((line, plane)),
+            DMA(()),
+        ],
+        compiler_params=pltpu.CompilerParams(
+            vmem_limit_bytes=VMEM_LIMIT, collective_id=0, has_side_effects=True
+        ),
+    )(by_peer, panel)
     sketch, outbound = pl.pallas_call(
         product_kernel,
         out_shape=(
@@ -163,14 +405,26 @@
         ],
         compiler_params=params,
     )(tile_count, slot, row, tiles, fetched.reshape(nslots, depth, width))
-    inbound = lax.all_to_all(outbound, AXES, split_axis=0, concat_axis=0, tiled=True)
+    hops = pltpu.VMEM((2, line - 1) + panel.shape, jnp.bfloat16)
     gram = pl.pallas_call(
-        gram_kernel,
-        out_shape=jax.ShapeDtypeStruct((held, depth, width), jnp.float32),
+        functools.partial(reduce_kernel, line, rows, grp),
+        out_shape=jax.ShapeDtypeStruct(panel.shape, jnp.float32),
         in_specs=[SMEM, VMEM],
         out_specs=VMEM,
-        compiler_params=params,
-    )(asked, inbound.reshape(nslots, depth, width))
+        scratch_shapes=[
+            pltpu.VMEM(paired, jnp.bfloat16),
+            hops,
+            hops,
+            pltpu.VMEM((2,) + panel.shape, jnp.float32),
+            DMA((2, line - 1)),
+            DMA((2, line - 1)),
+            DMA((line, plane)),
+            DMA((line, plane)),
+        ],
+        compiler_params=pltpu.CompilerParams(
+            vmem_limit_bytes=VMEM_LIMIT, collective_id=1, has_side_effects=True
+        ),
+    )(asked, outbound.reshape(paired))
     return sketch, gram
 
 

time: 247 us -> 218 us (0.88)
  Pallas kernels: 22.9 us -> 210 us
  blocking collectives: 122 us -> 0 us
  waiting for transfers between devices: 93.7 us -> 0 us
  starting transfers between devices: 3.7 us -> 0 us
  local copies, waits for them, and re-layouts: 1.19 us -> 3.96 us
    pallas_call x2, Pallas kernels: 8.64 us -> 190 us  [the longest x1 98.2 us: per_device(): pl.pallas_call(functools.partial(reduce_kernel, line, rows, grp), out_sha...]
    all_to_all x2 -> x0, blocking collectives: 122 us -> none  [the longest x1 108 us: per_device(): lax.all_to_all(outbound, AXES, split_axis=0, concat_axis=0, tiled=True)]
    all_to_all x1 -> x0, waiting for transfers between devices: 93.7 us -> none  [per_device(): lax.all_to_all(outgoing, AXES, split_axis=0, concat_axis=0, tiled=True)]
    pallas_call x1, Pallas kernels: 14.3 us -> 20.6 us  [per_device(): pl.pallas_call(product_kernel, out_shape=(jax.ShapeDtypeStruct((RB_DEV, d...]
    all_to_all x1 -> x0, starting transfers between devices: 3.7 us -> none  [per_device(): lax.all_to_all(outgoing, AXES, split_axis=0, concat_axis=0, tiled=True)]
    unnamed x2 -> x1, local copies, waits for them, and re-layouts: 0.01 us -> 3.1 us
  transfers between devices with their start and end apart: 1 -> 0, of which waited for: 1 -> 0; matrix products, arithmetic and copies ran while one was open for 0% -> 0% of each run, Pallas kernels for 0% -> 0%
where the time goes in v2:
time: 218 us
  Pallas kernels  210 us (96%)
  local copies, waits for them, and re-layouts  3.96 us (2%)
  other arithmetic  2.38 us (1%)
    pallas_call x1, Pallas kernels, per_device(): pl.pallas_call(functools.partial(reduce_kernel, line, rows, grp), out_sha...  98.2 us
    pallas_call x1, Pallas kernels, per_device(): pl.pallas_call(functools.partial(fetch_kernel, line, rows, grp), out_shap...  91.5 us
    pallas_call x1, Pallas kernels, per_device(): pl.pallas_call(product_kernel, out_shape=(jax.ShapeDtypeStruct((RB_DEV, d...  20.6 us

profile of v2, /device:TPU:0, one launch (start us, length us, event | category | flops | bytes accessed | tf_op | source)
XLA Modules:
  0.0 218.0 jit_solution(3753615116190469271)
XLA Ops:
  1.3 0.9 select_reduce_fusion
  2.2 0.2 and_reduce_fusion
  2.4 0.1 select_reduce_fusion.1
  2.5 1.2 add_select_fusion
  3.7 0.1 reduce_min.12
  3.8 0.1 reduce_max.12
  3.9 0.1 copy.11
  3.9 0.6 pad.4.wanted
  4.6 91.5 %shard_map.77 = (bf16[4,8,2,128,256]{4,3,2,1,0:T(8,128)(2,1)}, s32[8,8,128]{2,1,0:T(8,128)}) custom-call(s32[8,8,128]{2,1,0:T(8,128)} %pad.4.wanted, bf16[16,128,256]{2,1,0:T(8,128)(2,1)} %panel.1), custom_call_target="tpu_custom_call" | custom-call | tf_op jit(solution)/shard_map/pallas_call | solution.py:360
  96.0 20.6 %shard_map.78 = (bf16[48,128,256]{2,1,0:T(8,128)(2,1)}, bf16[64,128,256]{2,1,0:T(8,128)(2,1)}) custom-call(s32[1]{0:T(128)} %copy.13.count, s32[128]{0:T(128)} %get-tuple-element.16.slot, s32[128]{0:T(128)} %get-tuple-element.17.row, bf16[128,128,128]{2,1,0:T(8,128)(2,1)} %tiles.1, bf16[64,128,256]{2,1,0:T(8,128)(2,1)} %bitcast.9), custom_call_target="tpu_custom_call" | custom-call | tf_op jit(solution)/shard_map/pallas_call | solution.py:384
  116.7 98.2 %shard_map.79 = f32[16,128,256]{2,1,0:T(8,128)} custom-call(s32[8,8,128]{2,1,0:T(8,128)} %get-tuple-element.8.ids, bf16[4,8,2,128,256]{4,3,2,1,0:T(8,128)(2,1)} %bitcast.8), custom_call_target="tpu_custom_call" | custom-call | tf_op jit(solution)/shard_map/pallas_call | solution.py:409
  214.9 3.1 %copy.14 = f32[16,128,256]{2,1,0:T(8,128)} copy(f32[16,128,256]{2,1,0:T(8,128)} %shard_map.79) | data formatting | bytes 4194304
  (5 shorter events, 0.0 us)

commit v3 on v2

v3 whole, which is shorter than its diff:
```python
import functools

import jax
import jax.numpy as jnp
from jax import lax
from jax.experimental import pallas as pl
from jax.experimental.pallas import tpu as pltpu
from jax.sharding import PartitionSpec as P

RB_DEV = 48
PAIR_CAP = 2
UNROLL = 4
CHUNKS = 4
AXES = ("rows", "grp")
VMEM_LIMIT = 60 * 1024 * 1024


def index_tables(tile_rows, tile_cols, tile_count, block_perm, devices, held):
    slots = tile_cols.shape[0]
    live = jnp.arange(slots, dtype=jnp.int32) < tile_count[0]
    blocks = jnp.arange(block_perm.shape[0], dtype=jnp.int32)
    stored = jnp.sum(jnp.where(tile_cols[:, None] == blocks[None, :], block_perm[None, :], 0), axis=1)
    owner = stored // held
    local = stored % held
    rank = jnp.any(
        live[None, :] & (owner[None, :] == owner[:, None]) & (local[None, :] < local[:, None]), axis=1
    ).astype(jnp.int32)
    mine = live[None, :] & (owner[None, :] == jnp.arange(devices, dtype=jnp.int32)[:, None])
    first = jnp.min(jnp.where(mine, local[None, :], held), axis=1)
    last = jnp.max(jnp.where(mine, local[None, :], -1), axis=1)
    wanted = jnp.stack(
        [jnp.where(last >= 0, first, -1), jnp.where(last > first, last, -1)], axis=-1
    ).astype(jnp.int32)
    slot = jnp.where(live, owner * PAIR_CAP + rank, devices * PAIR_CAP)
    row = jnp.where(live, tile_rows, RB_DEV)
    return wanted, slot.astype(jnp.int32), row.astype(jnp.int32)


LINE = 4
MESH = pl.DeviceIdType.MESH


class Place:
    def __init__(self, line, rows, grp):
        self.line, self.grp = line, grp
        self.plane_rows = rows // line
        self.plane = self.plane_rows * grp
        row = lax.axis_index("rows")
        self.z = row // self.plane_rows
        self.p = (row % self.plane_rows) * grp + lax.axis_index("grp")

    def device(self, z, p):
        return (z * self.plane_rows + p // self.grp, p % self.grp)

    def peer(self, i):
        return lax.rem(self.p + i, self.plane)

    def greet(self):
        barrier = pltpu.get_barrier_semaphore()
        for k in range(1, self.line):
            to = self.device(lax.rem(self.z + k, self.line), self.p)
            pl.semaphore_signal(barrier, inc=1, device_id=to, device_id_type=MESH)

        def signal(i, c):
            to = self.device(self.z, self.peer(i))
            pl.semaphore_signal(barrier, inc=1, device_id=to, device_id_type=MESH)
            return c

        lax.fori_loop(1, self.plane, signal, 0)
        pl.semaphore_wait(barrier, self.line - 1 + self.plane - 1)

    def inside(self, z):
        return (z >= 0) & (z < self.line)


def remote(src, dst, send, recv, to):
    return pltpu.make_async_remote_copy(
        src_ref=src, dst_ref=dst, send_sem=send, recv_sem=recv, device_id=to, device_id_type=MESH
    )


def fetch_kernel(line, rows, grp, wanted, panel, fetched, asked, *scratch):
    far, (ids, out, id_send, id_recv, z_send, z_recv, send, recv, local) = (
        scratch[: 2 * (line - 1) * CHUNKS],
        scratch[2 * (line - 1) * CHUNKS :],
    )
    at = Place(line, rows, grp)
    z, p, plane = at.z, at.p, at.plane
    at.greet()

    depth = panel.shape[1] // CHUNKS

    def part(n):
        return pl.ds(n * depth, depth)

    def unit(way, k, n):
        return panel.at[:, part(n)] if k == 0 else far[(way * (line - 1) + k - 1) * CHUNKS + n]

    def along(way, k, n):
        step = 1 if way == 0 else -1
        to = at.device(jnp.clip(z + step, 0, line - 1), p)
        sems = z_send.at[way, k - 1, n], z_recv.at[way, k - 1, n]
        return remote(unit(way, k - 1, n), unit(way, k, n), *sems, to)

    def source(way, k):
        return z - k if way == 0 else z + k

    def sends(way, k):
        return at.inside(z + (1 if way == 0 else -1)) & at.inside(source(way, k - 1))

    def id_copy(i, mine):
        q = at.peer(i)
        slot = p if mine else q
        return remote(wanted.at[q], asked.at[slot], id_send.at[q], id_recv.at[slot], at.device(z, q))

    def start_ids(i, c):
        id_copy(i, True).start()
        return c

    lax.fori_loop(1, plane, start_ids, 0)
    for n in range(CHUNKS):
        for way in range(2):
            pl.when(sends(way, 1))(lambda way=way, n=n: along(way, 1, n).start())
    asked[p] = wanted[p]

    def wait_ids(i, c):
        id_copy(i, False).wait()
        return c

    lax.fori_loop(1, plane, wait_ids, 0)
    to_smem = pltpu.make_async_copy(asked, ids, local)
    to_smem.start()
    to_smem.wait()

    def across(plane_z, q, n, slot):
        return remote(
            out.at[plane_z, n, q],
            fetched.at[plane_z, slot, :, part(n)],
            send.at[plane_z, n, q],
            recv.at[plane_z, n, slot],
            at.device(z, q),
        )

    def spread(plane_z, load, n):
        def pick(i, c):
            q = at.peer(i)
            for j in range(PAIR_CAP):
                out[plane_z, n, q, j] = load(jnp.maximum(ids[q, 0, plane_z * PAIR_CAP + j], 0))
            return c

        lax.fori_loop(1, plane, pick, 0)
        for j in range(PAIR_CAP):
            fetched[plane_z, p, j, part(n)] = load(
                jnp.maximum(ids[p, 0, plane_z * PAIR_CAP + j], 0)
            )

        def start(i, c):
            across(plane_z, at.peer(i), n, p).start()
            return c

        lax.fori_loop(1, plane, start, 0)

    for n in range(CHUNKS):
        spread(z, lambda block, n=n: panel[block, part(n)], n)
    for k, n in [(k, n) for k in range(1, line) for n in range(CHUNKS)]:
        for way in range(2):

            def pass_on(way=way, k=k, n=n):
                along(way, k, n).wait_recv()
                if k + 1 < line:
                    pl.when(sends(way, k + 1))(lambda: along(way, k + 1, n).start())

            pl.when(at.inside(source(way, k)))(pass_on)
        for way in range(2):

            def hand_out(way=way, k=k, n=n):
                held = unit(way, k, n)
                spread(source(way, k), lambda block: held[block], n)

            pl.when(at.inside(source(way, k)))(hand_out)
    for k, n in [(k, n) for k in range(1, line) for n in range(CHUNKS)]:
        for way in range(2):
            pl.when(sends(way, k))(lambda way=way, k=k, n=n: along(way, k, n).wait_send())

    def finish(i, c):
        q = at.peer(i)
        for plane_z in range(line):
            for n in range(CHUNKS):
                across(plane_z, q, n, q).wait()
        return c

    lax.fori_loop(1, plane, finish, 0)


def product_kernel(
    count, slot, row, tiles_in, fetched_in, sketch_out, outbound_out, tiles, fetched, sketch, outbound, sk, part, sem
):
    nslots, width = outbound.shape[0], outbound.shape[2]
    steps = (count[0] + UNROLL - 1) // UNROLL
    copy = pltpu.make_async_copy
    tile_copies = copy(tiles_in, tiles, sem.at[0])
    tile_copies.start()

    def clear(ref):
        def body(i, c):
            ref[i] = jnp.zeros(ref.shape[1:], ref.dtype)
            return c

        lax.fori_loop(0, ref.shape[0], body, 0)

    def forward(i, c):
        got = []
        for u in range(UNROLL):
            t = i * UNROLL + u
            block = fetched[jnp.minimum(slot[t], nslots - 1)]
            got.append(jnp.dot(tiles[t], block, preferred_element_type=jnp.float32))
        for u in range(UNROLL):
            r = row[i * UNROLL + u]
            sk[r] = sk[r] + got[u]
        return c

    def rounded(i, c):
        sketch[i] = sk[i].astype(sketch.dtype)
        return c

    def backward(i, c):
        got = []
        for u in range(UNROLL):
            t = i * UNROLL + u
            block = sketch[jnp.minimum(row[t], sketch.shape[0] - 1)]
            got.append(
                lax.dot_general(
                    tiles[t], block, (((0,), (0,)), ((), ())), preferred_element_type=jnp.float32
                )
            )
        for u in range(UNROLL):
            s = slot[i * UNROLL + u]
            part[s] = part[s] + got[u]
        return c

    for column in range(0, sketch_out.shape[2], width):
        columns = pl.ds(column, width)
        block_copies = copy(fetched_in.at[:, :, columns], fetched, sem.at[1])
        block_copies.start()
        clear(sk)
        clear(part)
        block_copies.wait()
        if column == 0:
            tile_copies.wait()
        lax.fori_loop(0, steps, forward, 0)
        lax.fori_loop(0, sketch.shape[0], rounded, 0)
        sketch_copies = copy(sketch, sketch_out.at[:, :, columns], sem.at[2])
        sketch_copies.start()
        lax.fori_loop(0, steps, backward, 0)
        group = nslots // 4
        out_copies = []
        for n in range(4):

            def send_form(i, c):
                outbound[i] = part[i].astype(outbound.dtype)
                return c

            lax.fori_loop(n * group, (n + 1) * group, send_form, 0)
            piece = pl.ds(n * group, group)
            out_copies.append(
                copy(outbound.at[piece], outbound_out.at[piece, :, columns], sem.at[3 + n])
            )
            out_copies[-1].start()
        sketch_copies.wait()
        for done in out_copies:
            done.wait()


def reduce_kernel(line, rows, grp, ids, outbound, gram, inb, came, gone, total, z_send, z_recv, send, recv):
    at = Place(line, rows, grp)
    z, p, plane = at.z, at.p, at.plane
    held = gram.shape[0]
    depth = gram.shape[1] // CHUNKS

    def part(n):
        return pl.ds(n * depth, depth)

    at.greet()

    def target(way, k):
        return z + k if way == 0 else z - k

    def along(way, k, n):
        to = at.device(jnp.clip(target(way, 1), 0, line - 1), p)
        return remote(
            gone.at[way, k - 1, n],
            came.at[way, k - 1, n],
            z_send.at[way, k - 1, n],
            z_recv.at[way, k - 1, n],
            to,
        )

    def across(plane_z, q, n, slot):
        return remote(
            outbound.at[plane_z, q, :, part(n)],
            inb.at[plane_z, n, slot],
            send.at[plane_z, n, q],
            recv.at[plane_z, n, slot],
            at.device(z, q),
        )

    def begin(plane_z, n):
        def start(i, c):
            across(plane_z, at.peer(i), n, p).start()
            return c

        lax.fori_loop(1, plane, start, 0)
        for j in range(PAIR_CAP):
            inb[plane_z, n, p, j] = outbound[plane_z, p, j, part(n)]

    def add_up(plane_z, n, into):
        def arrive(i, c):
            q = at.peer(i)
            across(plane_z, q, n, q).wait()
            return c

        lax.fori_loop(1, plane, arrive, 0)

        def block(b, c):
            def term(q, acc):
                for j in range(PAIR_CAP):
                    hit = ids[q, 0, plane_z * PAIR_CAP + j] == b
                    acc = acc + jnp.where(hit, inb[plane_z, n, q, j].astype(jnp.float32), 0.0)
                return acc

            zero = jnp.zeros((depth, gram.shape[2]), jnp.float32)
            into[b, part(n)] = lax.fori_loop(0, plane, term, zero, unroll=8)
            return c

        lax.fori_loop(0, held, block, 0)

    stages = [
        (way, k, n) for k in range(line - 1, 0, -1) for n in range(CHUNKS) for way in range(2)
    ]
    for way, k, n in stages:
        pl.when(at.inside(target(way, k)))(lambda way=way, k=k, n=n: begin(target(way, k), n))
    for n in range(CHUNKS):
        begin(z, n)
    for k, n in [(k, n) for k in range(line - 1, 0, -1) for n in range(CHUNKS)]:
        for way in range(2):
            pl.when(at.inside(target(way, k)))(
                lambda way=way, k=k, n=n: add_up(target(way, k), n, total.at[way])
            )
        for way in range(2):
            has = at.inside(target(way, -1))

            def joined(way=way, k=k, n=n):
                along(way, k + 1, n).wait_recv()

                def block(b, c):
                    gone[way, k - 1, n, b] = (
                        total[way, b, part(n)] + came[way, k, n, b].astype(jnp.float32)
                    ).astype(gone.dtype)
                    return c

                lax.fori_loop(0, held, block, 0)

            def alone(way=way, k=k, n=n):
                def block(b, c):
                    gone[way, k - 1, n, b] = total[way, b, part(n)].astype(gone.dtype)
                    return c

                lax.fori_loop(0, held, block, 0)

            def stage(way=way, k=k, n=n, has=has, joined=joined, alone=alone):
                if k + 1 < line:
                    pl.when(has)(joined)
                    pl.when(jnp.logical_not(has))(alone)
                else:
                    alone()
                along(way, k, n).start()

            pl.when(at.inside(target(way, k)))(stage)
    for n in range(CHUNKS):
        add_up(z, n, gram)
    for n in range(CHUNKS):
        for way in range(2):

            def last(way=way, n=n):
                along(way, 1, n).wait_recv()

                def block(b, c):
                    gram[b, part(n)] = gram[b, part(n)] + came[way, 0, n, b].astype(jnp.float32)
                    return c

                lax.fori_loop(0, held, block, 0)

            pl.when(at.inside(target(way, -1)))(last)
    for way, k, n in stages:
        pl.when(at.inside(target(way, k)))(lambda way=way, k=k, n=n: along(way, k, n).wait_send())


SMEM = pl.BlockSpec(memory_space=pltpu.SMEM)
VMEM = pl.BlockSpec(memory_space=pltpu.VMEM)
ANY = pl.BlockSpec(memory_space=pl.ANY)
DMA = pltpu.SemaphoreType.DMA


def per_device(tiles, tile_rows, tile_cols, tile_count, block_perm, panel):
    rows, grp = lax.axis_size("rows"), lax.axis_size("grp")
    devices = rows * grp
    line = LINE if rows % LINE == 0 else rows
    plane = devices // line
    held, depth, width = panel.shape
    nslots = devices * PAIR_CAP
    part = width if nslots <= tiles.shape[0] else width // 2
    wanted, slot, row = index_tables(tile_rows, tile_cols, tile_count, block_perm, devices, held)
    by_peer = wanted.reshape(line, plane, PAIR_CAP).transpose(1, 0, 2).reshape(plane, 1, line * PAIR_CAP)
    by_peer = jnp.pad(by_peer, ((0, 0), (0, 7), (0, 128 - line * PAIR_CAP)))
    paired = (line, plane, PAIR_CAP, depth, width)
    unit = pltpu.VMEM((held, depth // CHUNKS, width), panel.dtype)
    cut = (line, CHUNKS, plane, PAIR_CAP, depth // CHUNKS, width)
    params = pltpu.CompilerParams(vmem_limit_bytes=VMEM_LIMIT)
    fetched, asked = pl.pallas_call(
        functools.partial(fetch_kernel, line, rows, grp),
        out_shape=(
            jax.ShapeDtypeStruct(paired, panel.dtype),
            jax.ShapeDtypeStruct(by_peer.shape, jnp.int32),
        ),
        in_specs=[VMEM, VMEM],
        out_specs=(VMEM, VMEM),
        scratch_shapes=[unit] * (2 * (line - 1) * CHUNKS)
        + [
            pltpu.SMEM(by_peer.shape, jnp.int32),
            pltpu.VMEM(cut, panel.dtype),
            DMA((plane,)),
            DMA((plane,)),
            DMA((2, line - 1, CHUNKS)),
            DMA((2, line - 1, CHUNKS)),
            DMA((line, CHUNKS, plane)),
            DMA((line, CHUNKS, plane)),
            DMA(()),
        ],
        compiler_params=pltpu.CompilerParams(
            vmem_limit_bytes=VMEM_LIMIT, collective_id=0, has_side_effects=True
        ),
    )(by_peer, panel)
    sketch, outbound = pl.pallas_call(
        product_kernel,
        out_shape=(
            jax.ShapeDtypeStruct((RB_DEV, depth, width), jnp.bfloat16),
            jax.ShapeDtypeStruct((nslots, depth, width), jnp.bfloat16),
        ),
        in_specs=[SMEM, SMEM, SMEM, ANY, ANY],
        out_specs=(ANY, ANY),
        scratch_shapes=[
            pltpu.VMEM(tiles.shape, tiles.dtype),
            pltpu.VMEM((nslots, depth, part), panel.dtype),
            pltpu.VMEM((RB_DEV, depth, part), jnp.bfloat16),
            pltpu.VMEM((nslots, depth, part), jnp.bfloat16),
            pltpu.VMEM((RB_DEV + 1, depth, part), jnp.float32),
            pltpu.VMEM((nslots + 1, depth, part), jnp.float32),
            DMA((7,)),
        ],
        compiler_params=params,
    )(tile_count, slot, row, tiles, fetched.reshape(nslots, depth, width))
    hops = pltpu.VMEM((2, line - 1, CHUNKS, held, depth // CHUNKS, width), jnp.bfloat16)
    gram = pl.pallas_call(
        functools.partial(reduce_kernel, line, rows, grp),
        out_shape=jax.ShapeDtypeStruct(panel.shape, jnp.float32),
        in_specs=[SMEM, VMEM],
        out_specs=VMEM,
        scratch_shapes=[
            pltpu.VMEM(cut, jnp.bfloat16),
            hops,
            hops,
            pltpu.VMEM((2,) + panel.shape, jnp.float32),
            DMA((2, line - 1, CHUNKS)),
            DMA((2, line - 1, CHUNKS)),
            DMA((line, CHUNKS, plane)),
            DMA((line, CHUNKS, plane)),
        ],
        compiler_params=pltpu.CompilerParams(
            vmem_limit_bytes=VMEM_LIMIT, collective_id=1, has_side_effects=True
        ),
    )(asked, outbound.reshape(paired))
    return sketch, gram


def solution(mesh):
    spec = P(AXES, None, None)
    return jax.shard_map(
        per_device,
        mesh=mesh,
        in_specs=(spec, P(AXES), P(AXES), P(AXES), P(), spec),
        out_specs=(spec, spec),
        check_vma=False,
    )
```

time: 218 us -> 196 us (0.90); the launches traced: 218 us -> 193 us
  Pallas kernels: 210 us -> 185 us
    pallas_call x1, Pallas kernels: 20.6 us -> 11.3 us  [per_device(): pl.pallas_call(product_kernel, out_shape=(jax.ShapeDtypeStruct((RB_DEV, d...]
    pallas_call x1, Pallas kernels: 98.2 us -> 90 us  [per_device(): pl.pallas_call(functools.partial(reduce_kernel, line, rows, grp), out_sha...]
    pallas_call x1, Pallas kernels: 91.5 us -> 84 us  [per_device(): pl.pallas_call(functools.partial(fetch_kernel, line, rows, grp), out_shap...]
where the time goes in v3:
time: 196 us; the launch traced here: 193 us
  Pallas kernels  185 us (94%)
  local copies, waits for them, and re-layouts  3.96 us (2%)
  other arithmetic  2.38 us (1%)
    pallas_call x1, Pallas kernels, per_device(): pl.pallas_call(functools.partial(reduce_kernel, line, rows, grp), out_sha...  90 us
    pallas_call x1, Pallas kernels, per_device(): pl.pallas_call(functools.partial(fetch_kernel, line, rows, grp), out_shap...  84 us
    pallas_call x1, Pallas kernels, per_device(): pl.pallas_call(product_kernel, out_shape=(jax.ShapeDtypeStruct((RB_DEV, d...  11.3 us

profile of v3, /device:TPU:0, one launch (start us, length us, event | category | flops | bytes accessed | tf_op | source)
XLA Modules:
  0.0 193.0 jit_solution(3210571608679816278)
XLA Ops:
  1.3 0.9 select_reduce_fusion
  2.2 0.2 and_reduce_fusion
  2.4 0.1 select_reduce_fusion.1
  2.5 1.2 add_select_fusion
  3.7 0.1 reduce_min.12
  3.8 0.1 reduce_max.12
  3.9 0.1 copy.11
  3.9 0.6 pad.4.wanted
  4.6 84.0 %shard_map.77 = (bf16[4,8,2,128,256]{4,3,2,1,0:T(8,128)(2,1)}, s32[8,8,128]{2,1,0:T(8,128)}) custom-call(s32[8,8,128]{2,1,0:T(8,128)} %pad.4.wanted, bf16[16,128,256]{2,1,0:T(8,128)(2,1)} %panel.1), custom_call_target="tpu_custom_call" | custom-call | tf_op jit(solution)/shard_map/pallas_call | solution.py:419
  88.6 11.3 %shard_map.78 = (bf16[48,128,256]{2,1,0:T(8,128)(2,1)}, bf16[64,128,256]{2,1,0:T(8,128)(2,1)}) custom-call(s32[1]{0:T(128)} %copy.13.count, s32[128]{0:T(128)} %get-tuple-element.16.slot, s32[128]{0:T(128)} %get-tuple-element.17.row, bf16[128,128,128]{2,1,0:T(8,128)(2,1)} %tiles_in.1, bf16[64,128,256]{2,1,0:T(8,128)(2,1)} %bitcast.9), custom_call_target="tpu_custom_call" | custom-call | tf_op jit(solution)/shard_map/pallas_call | solution.py:443
  99.9 90.0 %shard_map.79 = f32[16,128,256]{2,1,0:T(8,128)} custom-call(s32[8,8,128]{2,1,0:T(8,128)} %get-tuple-element.8.ids, bf16[4,8,2,128,256]{4,3,2,1,0:T(8,128)(2,1)} %bitcast.8), custom_call_target="tpu_custom_call" | custom-call | tf_op jit(solution)/shard_map/pallas_call | solution.py:463
  189.9 3.1 %copy.14 = f32[16,128,256]{2,1,0:T(8,128)} copy(f32[16,128,256]{2,1,0:T(8,128)} %shard_map.79) | data formatting | bytes 4194304
  (5 shorter events, 0.0 us)

commit v4 on v3

--- a/solution.py
+++ b/solution.py
@@ -11,6 +11,7 @@
 PAIR_CAP = 2
 UNROLL = 4
 CHUNKS = 4
+PIECES = 4
 AXES = ("rows", "grp")
 VMEM_LIMIT = 60 * 1024 * 1024
 
@@ -141,6 +142,11 @@
             at.device(z, q),
         )
 
+    def keep(plane_z, n):
+        return pltpu.make_async_copy(
+            out.at[plane_z, n, p], fetched.at[plane_z, p, :, part(n)], send.at[plane_z, n, p]
+        )
+
     def spread(plane_z, load, n):
         def pick(i, c):
             q = at.peer(i)
@@ -150,15 +156,14 @@
 
         lax.fori_loop(1, plane, pick, 0)
         for j in range(PAIR_CAP):
-            fetched[plane_z, p, j, part(n)] = load(
-                jnp.maximum(ids[p, 0, plane_z * PAIR_CAP + j], 0)
-            )
+            out[plane_z, n, p, j] = load(jnp.maximum(ids[p, 0, plane_z * PAIR_CAP + j], 0))
 
         def start(i, c):
             across(plane_z, at.peer(i), n, p).start()
             return c
 
         lax.fori_loop(1, plane, start, 0)
+        keep(plane_z, n).start()
 
     for n in range(CHUNKS):
         spread(z, lambda block, n=n: panel[block, part(n)], n)
@@ -190,6 +195,9 @@
         return c
 
     lax.fori_loop(1, plane, finish, 0)
+    for plane_z in range(line):
+        for n in range(CHUNKS):
+            keep(plane_z, n).wait()
 
 
 def product_kernel(
@@ -198,8 +206,11 @@
     nslots, width = outbound.shape[0], outbound.shape[2]
     steps = (count[0] + UNROLL - 1) // UNROLL
     copy = pltpu.make_async_copy
-    tile_copies = copy(tiles_in, tiles, sem.at[0])
-    tile_copies.start()
+    group_steps = tiles.shape[0] // UNROLL // PIECES
+    tile_copies = []
+    for n in range(PIECES):
+        piece = pl.ds(n * group_steps * UNROLL, group_steps * UNROLL)
+        tile_copies.append(copy(tiles_in.at[piece], tiles.at[piece], sem.at[6 + n]))
 
     def clear(ref):
         def body(i, c):
@@ -240,16 +251,22 @@
 
     for column in range(0, sketch_out.shape[2], width):
         columns = pl.ds(column, width)
-        block_copies = copy(fetched_in.at[:, :, columns], fetched, sem.at[1])
+        block_copies = copy(fetched_in.at[:, :, columns], fetched, sem.at[0])
         block_copies.start()
+        if column == 0:
+            for load in tile_copies:
+                load.start()
         clear(sk)
         clear(part)
         block_copies.wait()
-        if column == 0:
-            tile_copies.wait()
-        lax.fori_loop(0, steps, forward, 0)
+        for n in range(PIECES):
+            if column == 0:
+                tile_copies[n].wait()
+            first = jnp.minimum(steps, n * group_steps)
+            last = jnp.minimum(steps, (n + 1) * group_steps)
+            lax.fori_loop(first, last, forward, 0)
         lax.fori_loop(0, sketch.shape[0], rounded, 0)
-        sketch_copies = copy(sketch, sketch_out.at[:, :, columns], sem.at[2])
+        sketch_copies = copy(sketch, sketch_out.at[:, :, columns], sem.at[1])
         sketch_copies.start()
         lax.fori_loop(0, steps, backward, 0)
         group = nslots // 4
@@ -263,7 +280,7 @@
             lax.fori_loop(n * group, (n + 1) * group, send_form, 0)
             piece = pl.ds(n * group, group)
             out_copies.append(
-                copy(outbound.at[piece], outbound_out.at[piece, :, columns], sem.at[3 + n])
+                copy(outbound.at[piece], outbound_out.at[piece, :, columns], sem.at[2 + n])
             )
             out_copies[-1].start()
         sketch_copies.wait()
@@ -304,14 +321,18 @@
             at.device(z, q),
         )
 
+    def keep(plane_z, n):
+        return pltpu.make_async_copy(
+            outbound.at[plane_z, p, :, part(n)], inb.at[plane_z, n, p], send.at[plane_z, n, p]
+        )
+
     def begin(plane_z, n):
         def start(i, c):
             across(plane_z, at.peer(i), n, p).start()
             return c
 
         lax.fori_loop(1, plane, start, 0)
-        for j in range(PAIR_CAP):
-            inb[plane_z, n, p, j] = outbound[plane_z, p, j, part(n)]
+        keep(plane_z, n).start()
 
     def add_up(plane_z, n, into):
         def arrive(i, c):
@@ -320,6 +341,7 @@
             return c
 
         lax.fori_loop(1, plane, arrive, 0)
+        keep(plane_z, n).wait()
 
         def block(b, c):
             def term(q, acc):
@@ -423,7 +445,7 @@
             jax.ShapeDtypeStruct(by_peer.shape, jnp.int32),
         ),
         in_specs=[VMEM, VMEM],
-        out_specs=(VMEM, VMEM),
+        out_specs=(ANY, VMEM),
         scratch_shapes=[unit] * (2 * (line - 1) * CHUNKS)
         + [
             pltpu.SMEM(by_peer.shape, jnp.int32),
@@ -455,7 +477,7 @@
             pltpu.VMEM((nslots, depth, part), jnp.bfloat16),
             pltpu.VMEM((RB_DEV + 1, depth, part), jnp.float32),
             pltpu.VMEM((nslots + 1, depth, part), jnp.float32),
-            DMA((7,)),
+            DMA((6 + PIECES,)),
         ],
         compiler_params=params,
     )(tile_count, slot, row, tiles, fetched.reshape(nslots, depth, width))
@@ -463,7 +485,7 @@
     gram = pl.pallas_call(
         functools.partial(reduce_kernel, line, rows, grp),
         out_shape=jax.ShapeDtypeStruct(panel.shape, jnp.float32),
-        in_specs=[SMEM, VMEM],
+        in_specs=[SMEM, ANY],
         out_specs=VMEM,
         scratch_shapes=[
             pltpu.VMEM(cut, jnp.bfloat16),

time: 196 us -> 193 us (0.985)
  Pallas kernels: 185 us -> 183 us
    pallas_call x1, Pallas kernels: 90 us -> 87.7 us  [per_device(): pl.pallas_call(functools.partial(reduce_kernel, line, rows, grp), out_sha...]
where the time goes in v4:
time: 193 us; the launch traced here: 191 us
  Pallas kernels  183 us (95%)
  local copies, waits for them, and re-layouts  3.96 us (2%)
  other arithmetic  2.38 us (1%)
    pallas_call x1, Pallas kernels, per_device(): pl.pallas_call(functools.partial(reduce_kernel, line, rows, grp), out_sha...  87.7 us
    pallas_call x1, Pallas kernels, per_device(): pl.pallas_call(functools.partial(fetch_kernel, line, rows, grp), out_shap...  82.8 us
    pallas_call x1, Pallas kernels, per_device(): pl.pallas_call(product_kernel, out_shape=(jax.ShapeDtypeStruct((RB_DEV, d...  12.8 us

profile of v4, /device:TPU:0, one launch (start us, length us, event | category | flops | bytes accessed | tf_op | source)
XLA Modules:
  0.0 191.0 jit_solution(16114381545847472003)
XLA Ops:
  1.3 0.9 select_reduce_fusion
  2.2 0.2 and_reduce_fusion
  2.4 0.1 select_reduce_fusion.1
  2.5 1.2 add_select_fusion
  3.7 0.1 reduce_min.12
  3.8 0.1 reduce_max.12
  3.9 0.1 copy.11
  3.9 0.6 pad.4.wanted
  4.6 82.8 %shard_map.77 = (bf16[4,8,2,128,256]{4,3,2,1,0:T(8,128)(2,1)}, s32[8,8,128]{2,1,0:T(8,128)}) custom-call(s32[8,8,128]{2,1,0:T(8,128)} %pad.4.wanted, bf16[16,128,256]{2,1,0:T(8,128)(2,1)} %panel.1), custom_call_target="tpu_custom_call" | custom-call | tf_op jit(solution)/shard_map/pallas_call | solution.py:441
  87.4 12.8 %shard_map.78 = (bf16[48,128,256]{2,1,0:T(8,128)(2,1)}, bf16[64,128,256]{2,1,0:T(8,128)(2,1)}) custom-call(s32[1]{0:T(128)} %copy.13.count, s32[128]{0:T(128)} %get-tuple-element.16.slot, s32[128]{0:T(128)} %get-tuple-element.17.row, bf16[128,128,128]{2,1,0:T(8,128)(2,1)} %tiles_in.1, bf16[64,128,256]{2,1,0:T(8,128)(2,1)} %bitcast.9), custom_call_target="tpu_custom_call" | custom-call | tf_op jit(solution)/shard_map/pallas_call | solution.py:465
  100.2 87.7 %shard_map.79 = f32[16,128,256]{2,1,0:T(8,128)} custom-call(s32[8,8,128]{2,1,0:T(8,128)} %get-tuple-element.8.ids, bf16[4,8,2,128,256]{4,3,2,1,0:T(8,128)(2,1)} %bitcast.8), custom_call_target="tpu_custom_call" | custom-call | tf_op jit(solution)/shard_map/pallas_call | solution.py:485
  187.9 3.1 %copy.14 = f32[16,128,256]{2,1,0:T(8,128)} copy(f32[16,128,256]{2,1,0:T(8,128)} %shard_map.79) | data formatting | bytes 4194304
  (5 shorter events, 0.0 us)
